TPU v7x, 128 devices: a whole 4x4x4 slice. The times are simulated.
128 devices in a mesh: gx: 4 (over x_lo, core), gy: 4 (over z), gz: 8 (over x_hi, y).
Axes of the slice: x: 4 (x_hi: 2, x_lo: 2; x = x_hi * 2 + x_lo), y: 4, z: 4, core: 2. Of those that a mesh axis runs over, the one named last changes fastest.
Arguments:
- fields: float32 [11, 500, 32, 1024], P(None, 'gx', 'gy', 'gz'), may hold values from -6 to 6
- var_scale: float32 [11], replicated, may hold values from 0.3 to 3
- start_basis: float32 [500, 64], replicated, may hold values from -6 to 6
Outputs:
- factor: float32 [500, 64], replicated
- core: float32 [64, 11, 32, 1024], P('gx', None, 'gy', 'gz')
All inputs are finite; a program needn't handle non-finite values.
Results may differ from a plain program's by a relative error of at most 0.0002.
Values sent between devices are 32-bit elements; how exact they have to be, the bound alone decides.
A program may use at most 128 MiB of HBM per device.

v0:
```python
import jax
import jax.numpy as jnp
from jax import lax
from jax.sharding import PartitionSpec as P

ITERS = 3


def orthonormal(block):
    small = jnp.dot(block.T, block, precision=lax.Precision.HIGHEST)
    lower = jnp.linalg.cholesky(small)
    return jax.scipy.linalg.solve_triangular(lower, block.T, lower=True).T


def per_device(fields, var_scale, start_basis):
    scaled = fields * var_scale[:, None, None, None]
    contract = (((0, 2, 3), (0, 2, 3)), ((), ()))
    swapped = lax.all_to_all(scaled, "gx", split_axis=2, concat_axis=1, tiled=True)
    partial_gram = lax.dot_general(swapped, swapped, contract, precision=lax.Precision.HIGHEST)
    gram = lax.psum(partial_gram, ("gx", "gy", "gz"))
    basis = start_basis
    for step in range(ITERS):
        basis = orthonormal(jnp.dot(gram, basis, precision=lax.Precision.HIGHEST))
    along_rows = (((0,), (1,)), ((), ()))
    full_core = lax.dot_general(basis, swapped, along_rows, precision=lax.Precision.HIGHEST)
    core = lax.all_to_all(full_core, "gx", split_axis=0, concat_axis=2, tiled=True)
    return (basis, core)


def solution(mesh):
    in_specs = (P(None, "gx", "gy", "gz"), P(), P())
    out_specs = (P(), P("gx", None, "gy", "gz"))
    return jax.shard_map(
        per_device, mesh=mesh, in_specs=in_specs, out_specs=out_specs, check_vma=False
    )
```

profile of v0, /device:TPU:1, one launch (start us, length us, event | category | flops | bytes accessed | tf_op | source)
XLA Modules:
  0.0 325.3 jit_solution(2125841500169065226)
XLA Ops:
  7.2 3.1 broadcast_multiply_fusion
  10.3 1.1 copy.22
  11.4 68.0 %all_to_all.36 = f32[11,125,8,128]{3,1,0,2:T(8,128)S(1)} all-to-all(f32[11,125,8,128]{3,1,0,2:T(8,128)S(1)} %copy.22), channel_id=1, replica_groups=mesh['gx'=4,'gy'=4,'gz'=8] {'gx'}, dimensions={2} | all-to-all | bytes 11264000 | tf_op jit(solution)/shard_map/all_to_all | solution.py:18
  79.4 2.9 copy.32
  82.3 6.2 %all_to_all.29 = f32[11,500,2,128]{3,1,2,0:T(8,128)} reshape(f32[11,4,125,2,128]{4,2,1,3,0:T(8,128)} %bitcast.72) | data formatting | bytes 11264000 | tf_op jit(solution)/shard_map/all_to_all | solution.py:18
  88.5 13.6 %convolution_bitcast_fusion = f32[500,500]{1,0:T(8,128)} fusion(f32[11,500,2,128]{3,1,2,0:T(8,128)} %all_to_all.29), kind=kOutput, calls=%fused_computation.2 | convolution fusion | flops 8448000000 | bytes 6632000 | tf_op jit(solution)/shard_map/dot_general | solution.py:19
  102.1 151.0 %all-reduce.2.cloned.1.call-done = f32[500,500]{1,0:T(8,128)} async-done(((f32[500,500]{1,0:T(8,128)}), f32[500,500]{1,0:T(8,128)}) %all-reduce.2.cloned.1.call-update) | async-done | bytes 1000016 | tf_op jit(solution)/shard_map/psum | solution.py:20
  253.1 2.3 fusion.21
  255.7 5.8 %cholesky.59 = f32[64,64]{1,0:T(8,128)S(1)} custom-call(f32[64,64]{1,0:T(8,128)S(1)} %fusion.16), custom_call_target="Cholesky" | custom-call | tf_op jit(solution)/shard_map/jit(cholesky)/cholesky | solution.py:11
  261.6 0.6 compare_reduce_fusion.2
  262.3 0.7 fusion.8
  262.9 4.9 %custom-call.7 = f32[1,64,64]{1,2,0:T(8,128)S(1)} custom-call(f32[1,64,64]{2,1,0:T(8,128)S(1)} %fusion.8), custom_call_target="InvertDiagBlocksLowerTriangular" | custom-call | tf_op jit(solution)/shard_map/jit(_solve_triangular)/triangular_solve | solution.py:12
  268.2 2.3 fusion.23
  270.8 5.8 %cholesky.70 = f32[64,64]{1,0:T(8,128)S(1)} custom-call(f32[64,64]{1,0:T(8,128)S(1)} %fusion.14), custom_call_target="Cholesky" | custom-call | tf_op jit(solution)/shard_map/jit(cholesky)/cholesky | solution.py:11
  276.7 0.6 compare_reduce_fusion.1
  277.3 0.7 fusion.9
  278.0 4.9 %custom-call.8 = f32[1,64,64]{1,2,0:T(8,128)S(1)} custom-call(f32[1,64,64]{2,1,0:T(8,128)S(1)} %fusion.9), custom_call_target="InvertDiagBlocksLowerTriangular" | custom-call | tf_op jit(solution)/shard_map/jit(_solve_triangular)/triangular_solve | solution.py:12
  283.2 2.3 fusion.25
  285.9 5.8 %cholesky.81 = f32[64,64]{1,0:T(8,128)S(1)} custom-call(f32[64,64]{1,0:T(8,128)S(1)} %fusion.12), custom_call_target="Cholesky" | custom-call | tf_op jit(solution)/shard_map/jit(cholesky)/cholesky | solution.py:11
  292.4 0.7 fusion.10
  293.1 4.9 %custom-call.9 = f32[1,64,64]{1,2,0:T(8,128)S(1)} custom-call(f32[1,64,64]{2,1,0:T(8,128)S(1)} %fusion.10), custom_call_target="InvertDiagBlocksLowerTriangular" | custom-call | tf_op jit(solution)/shard_map/jit(_solve_triangular)/triangular_solve | solution.py:12
  298.3 6.1 %fusion = f32[64,11,2,128]{3,0,2,1:T(8,128)S(1)} fusion(f32[11,500,2,128]{3,1,2,0:T(8,128)} %all_to_all.29, f32[64,500]{1,0:T(8,128)S(1)} %fusion.2), kind=kOutput, calls=%fused_computation.3 | convolution fusion | flops 1081344000 | bytes 6480896 | tf_op jit(solution)/shard_map/dot_general | solution.py:25
  305.0 12.3 %all_to_all.37 = f32[64,11,2,128]{3,2,1,0:T(2,128)S(1)} all-to-all(f32[64,11,2,128]{3,2,1,0:T(2,128)S(1)} %copy.27), channel_id=1, replica_groups=mesh['gx'=4,'gy'=4,'gz'=8] {'gx'}, dimensions={0} | all-to-all | bytes 1441792 | tf_op jit(solution)/shard_map/all_to_all | solution.py:26
  317.3 1.1 copy.28
  (23 shorter events, 3.4 us)
Async XLA Ops:
  7.2 245.9 %copy-start = (f32[500,64]{0,1:T(8,128)S(1)}, f32[500,64]{0,1:T(8,128)}, u32[]{:S(2)}) copy-start(f32[500,64]{0,1:T(8,128)} %param.8) | copy-start | bytes 384004
  7.2 245.9 %all-reduce.2.cloned.1.call-start = ((), (), s32[]{:S(2)}) async-start(), calls=%async_computation.2 | async-start | bytes 2064384 | tf_op jit(solution)/shard_map/psum | solution.py:20
  298.3 20.1 %copy-start.1 = (f32[64,500]{1,0:T(8,128)}, f32[64,500]{1,0:T(8,128)S(1)}, u32[]{:S(2)}) copy-start(f32[64,500]{1,0:T(8,128)S(1)} %fusion.2) | copy-start | bytes 384004
Sparse Core Ops, SparseCore 0:
  102.3 150.8 all-reduce.1
where the time goes:
time: 326 us; the launch traced here: 325 us
  waiting for transfers between devices  151 us (46%)
  blocking collectives  80.3 us (25%)
  other arithmetic  39.3 us (12%)
  matrix products  28.4 us (9%)
  between operations  14.2 us (4%)
  local copies, waits for them, and re-layouts  12.1 us (4%)
    psum x1, waiting for transfers between devices, per_device(): gram = lax.psum(partial_gram, ('gx', 'gy', 'gz'))  151 us
    all_to_all x1, blocking collectives, per_device(): lax.all_to_all(scaled, 'gx', split_axis=2, concat_axis=1, tiled=True)  68 us
    another operation x9, other arithmetic, orthonormal(): lower = jnp.linalg.cholesky(small)  19.6 us
    another operation x6, other arithmetic, orthonormal(): return jax.scipy.linalg.solve_triangular(lower, block.T, lower=True).T  16.6 us
    dot_general x1, matrix products, per_device(): lax.dot_general(swapped, swapped, contract, precision=lax.Precision.HIGHEST)  13.6 us
    all_to_all x1, blocking collectives, per_device(): lax.all_to_all(full_core, 'gx', split_axis=0, concat_axis=2, tiled=True)  12.3 us
    all_to_all x2, local copies, waits for them, and re-layouts, per_device(): lax.all_to_all(scaled, 'gx', split_axis=2, concat_axis=1, tiled=True)  9.05 us
    dot_general x3, matrix products, per_device(): basis = orthonormal(jnp.dot(gram, basis, precision=lax.Precision.HIGHEST))  6.83 us
  transfers between devices with their start and end apart: 1, of which 1 were waited for; matrix products, arithmetic and copies ran while one was open for 0% of the time, Pallas kernels for 0%

commit v1 on v0

v1 whole, which is shorter than its diff:
```python
import functools

import jax
import jax.numpy as jnp
from jax import lax
from jax.experimental import pallas as pl
from jax.experimental.pallas import tpu as pltpu
from jax.sharding import PartitionSpec as P

ITERS = 3
MESH = pl.DeviceIdType.MESH
NN = (((1,), (0,)), ((), ()))
NT = (((1,), (1,)), ((), ()))
F32 = jnp.float32
BF16 = jnp.bfloat16
HI = lax.Precision.HIGHEST


def split(x):
    hi = x.astype(BF16)
    return hi, (x - hi.astype(F32)).astype(BF16)


def dot(a, b, dims):
    return lax.dot_general(a, b, dims, preferred_element_type=F32)


def dot3(ah, al, bh, bl, dims):
    return dot(ah, bh, dims) + (dot(ah, bl, dims) + dot(al, bh, dims))


def column(block, j):
    return block.reshape(512, 128)[pl.ds(j, 128, stride=4), :]


def eliminate(m):
    tiles = [m[8 * t : 8 * t + 8, :] for t in range(8)]
    sub = lax.broadcasted_iota(jnp.int32, (8, 128), 0)
    for q in range(8):
        cols = [
            {t: jnp.broadcast_to(tiles[t][:, 8 * q + k : 8 * q + k + 1], (8, 128)) for t in range(q, 8)}
            for k in range(8)
        ]
        pivots = jnp.ones((8, 128), F32)
        for k in range(8):
            p = jnp.broadcast_to(cols[k][q][k : k + 1, :], (8, 128))
            rp = 1.0 / p
            row = jnp.broadcast_to(tiles[q][k : k + 1, :], (8, 128))
            across = {l: jnp.broadcast_to(cols[l][q][k : k + 1, :], (8, 128)) for l in range(k + 1, 8)}
            for t in range(q, 8):
                f = cols[k][t] * rp
                if t == q:
                    f = jnp.where(sub > k, f, 0.0)
                tiles[t] = tiles[t] - f * row
                for l in range(k + 1, 8):
                    cols[l][t] = cols[l][t] - f * across[l]
            pivots = jnp.where(sub == k, p, pivots)
        r = lax.rsqrt(pivots)
        r = r * (1.5 - 0.5 * (pivots * r) * r)
        tiles[q] = tiles[q] * r
    return jnp.concatenate(tiles, axis=0)


def kernel(
    nv, nz, ny, scale_ref, x_ref, start_ref,
    factor_ref, core_ref,
    xo, xd, xx, xf, Xh, Xl, Yh, Yl,
    acc_own, acc_ab,
    zb_o, b1_o, yb_o, b2_o, xb_o, zb_a, b1_a, yb_a, b2_a, xb_a,
    gd, gx_, gh, gl, bt, fh, fl, psend, precv,
    s_loc, s_d2d, s_x, s_fw, s_ro, s_ra, s_g, s_c,
):
    me = lax.axis_index("gx")
    z = lax.axis_index("gy")
    hy = lax.axis_index("gz")
    h = me // 2
    c = lax.rem(me, 2)
    o = 1 - h
    xh = hy // ny
    y = lax.rem(hy, ny)
    rz = 128 // nz
    ry = rz // ny

    def dev(gx=me, gy=z, xhi=xh, yy=y):
        return {"gx": gx, "gy": gy, "gz": xhi * ny + yy}

    mate = dev(gx=2 * h + (1 - c))
    across = dev(gx=2 * o + c)
    zs = [dev(gy=lax.rem(z + d, nz)) for d in range(1, nz)]
    ys = [dev(yy=lax.rem(y + d, ny)) for d in range(1, ny)]
    x_hi = dev(xhi=1 - xh)
    x_all = [x_hi, across, dev(gx=2 * o + c, xhi=1 - xh)]

    def rcopy(src, dst, sems, at, to):
        return pltpu.make_async_remote_copy(
            src_ref=src, dst_ref=dst, send_sem=sems.at[(0,) + at], recv_sem=sems.at[(1,) + at],
            device_id=to, device_id_type=MESH,
        )

    def local(v, half):
        return pltpu.make_async_copy(x_ref.at[v, :, half], xo.at[v, half, 0:125], s_loc.at[v, half])

    def c_d2d(v):
        return rcopy(xo.at[v, :, 0:125], xd.at[v, :, 0:125], s_d2d, (v,), mate)

    def c_x(v):
        return rcopy(xo.at[v, o, 0:125], xx.at[v, 0:125], s_x, (v,), across)

    def c_fw(v):
        return rcopy(xx.at[v, 0:125], xf.at[v, 0:125], s_fw, (v,), mate)

    for v in range(nv):
        local(v, o).start()
        local(v, h).start()

    barrier = pltpu.get_barrier_semaphore()
    greet = [mate] + zs + ys + x_all
    for d in greet:
        pl.semaphore_signal(barrier, inc=1, device_id=d, device_id_type=MESH)
    zero = jnp.zeros((3, 4, 128), F32)
    for v in range(nv):
        for half in range(2):
            xo[v, half, 125:128] = zero
            xd[v, half, 125:128] = zero
        xx[v, 125:128] = zero
        xf[v, 125:128] = zero
    pl.semaphore_wait(barrier, len(greet))

    @pl.loop(0, nv)
    def _(v):
        local(v, o).wait()
        c_x(v).start()
        local(v, h).wait()
        c_d2d(v).start()

    acc_own[...] = jnp.zeros_like(acc_own)
    acc_ab[...] = jnp.zeros_like(acc_ab)
    zrow = jnp.zeros((3, 64), F32)
    for g in range(4):
        part = jnp.concatenate([start_ref[125 * g : 125 * g + 125, :], zrow], axis=0)
        bt[:, 128 * g : 128 * g + 128] = part.T

    def convert(block, s, dh, dl):
        for j in range(4):
            hi, lo = split(column(block, j) * s)
            dh[:, 128 * j : 128 * j + 128] = hi
            dl[:, 128 * j : 128 * j + 128] = lo

    def rows(g, n=128):
        return pl.ds(pl.multiple_of(g * 128, 128), n)

    @pl.loop(0, nv)
    def _(v):
        s = scale_ref[v]
        convert(xo.at[v, h], s, Xh.at[v, rows(me)], Xl.at[v, rows(me)])
        convert(xo.at[v, o], s, Yh.at[rows(c)], Yl.at[rows(c)])
        c_d2d(v).wait_recv()
        m2 = 2 * h + (1 - c)
        convert(xd.at[v, h], s, Xh.at[v, rows(m2)], Xl.at[v, rows(m2)])
        convert(xd.at[v, o], s, Yh.at[rows(1 - c)], Yl.at[rows(1 - c)])
        chip = pl.ds(pl.multiple_of(h * 256, 256), 256)
        acc_own[...] += dot3(
            Xh[v, rows(me), :], Xl[v, rows(me), :], Xh[v, chip, :], Xl[v, chip, :], NT
        ) + dot3(Yh[rows(c), :], Yl[rows(c), :], Yh[...], Yl[...], NT)

    class Reduce:
        def __init__(self, acc, zb, b1, yb, b2, xb, out, sems, partners, slot, slots):
            self.acc, self.zb, self.b1, self.yb, self.b2, self.xb = acc, zb, b1, yb, b2, xb
            self.out, self.sems, self.partners, self.slot, self.slots = out, sems, partners, slot, slots

        def at(self, n, start):
            return pl.ds(pl.multiple_of(start, ry), n)

        def zc(self, d):
            to = lax.rem(z + d, nz)
            return rcopy(self.acc.at[self.at(rz, to * rz)], self.zb.at[d - 1], self.sems, (0, d - 1), zs[d - 1])

        def yc(self, d):
            to = lax.rem(y + d, ny)
            return rcopy(self.b1.at[self.at(ry, to * ry)], self.yb.at[d - 1], self.sems, (1, d - 1), ys[d - 1])

        def xc(self, k):
            return rcopy(self.b2, self.xb.at[self.slot], self.sems, (2, k), self.partners[k])

        def yg(self, d):
            here = self.out.at[self.at(ry, c * 128 + z * rz + y * ry)]
            return rcopy(here, here, self.sems, (3, d - 1), ys[d - 1])

        def zg(self, d):
            here = self.out.at[self.at(rz, c * 128 + z * rz)]
            return rcopy(here, here, self.sems, (4, d - 1), zs[d - 1])

        def s0(self):
            for d in range(1, nz):
                self.zc(d).start()

        def s1(self):
            for d in range(1, nz):
                self.zc(d).wait_recv()
            t = self.acc[self.at(rz, z * rz), :]
            for d in range(1, nz):
                t = t + self.zb[d - 1]
            self.b1[...] = t
            for d in range(1, ny):
                self.yc(d).start()

        def s2(self):
            for d in range(1, ny):
                self.yc(d).wait_recv()
            t = self.b1[self.at(ry, y * ry), :]
            for d in range(1, ny):
                t = t + self.yb[d - 1]
            self.b2[...] = t
            for k in range(len(self.partners)):
                self.xc(k).start()
            self.xb[self.slot] = t

        def s3(self):
            for k in range(len(self.partners)):
                self.xc(k).wait_recv()
            t = self.xb[0]
            for k in range(1, self.slots):
                t = t + self.xb[k]
            self.out[self.at(ry, c * 128 + z * rz + y * ry), :] = t
            for d in range(1, ny):
                self.yg(d).start()

        def s4(self):
            for d in range(1, ny):
                self.yg(d).wait_recv()
            for d in range(1, nz):
                self.zg(d).start()

        def s5(self):
            for d in range(1, nz):
                self.zg(d).wait_recv()

        def finish(self):
            for d in range(1, nz):
                self.zc(d).wait_send()
                self.zg(d).wait_send()
            for d in range(1, ny):
                self.yc(d).wait_send()
                self.yg(d).wait_send()
            for k in range(len(self.partners)):
                self.xc(k).wait_send()

    own = Reduce(acc_own, zb_o, b1_o, yb_o, b2_o, xb_o, gd.at[h], s_ro, [x_hi], xh, 2)
    ab = Reduce(acc_ab, zb_a, b1_a, yb_a, b2_a, xb_a, gx_, s_ra, x_all, xh * 2 + h, 4)

    own.s0()
    steps = {1: own.s1, 3: own.s2, 5: own.s3, 7: own.s4, 9: own.s5}

    @pl.loop(0, nv)
    def _(v):
        s = scale_ref[v]
        c_x(v).wait_recv()
        c_fw(v).start()
        g2 = 2 * o + c
        convert(xx.at[v], s, Xh.at[v, rows(g2)], Xl.at[v, rows(g2)])
        for k, f in steps.items():
            pl.when(v == k * nv // 11)(f)
        c_fw(v).wait_recv()
        g3 = 2 * o + (1 - c)
        convert(xf.at[v], s, Xh.at[v, rows(g3)], Xl.at[v, rows(g3)])
        acc_ab[...] += dot3(
            Xh[v, rows(c), :], Xl[v, rows(c), :], Xh[v, 256:512, :], Xl[v, 256:512, :], NT
        )

    mine = pl.ds(pl.multiple_of(c * 128, 128), 128)
    g_d2d = rcopy(gd.at[h, mine], gd.at[h, mine], s_g, (0,), mate)
    g_x = rcopy(gd.at[h, mine], gd.at[h, mine], s_g, (1,), across)
    g_got = rcopy(gd.at[o, mine], gd.at[o, mine], s_g, (1,), across)
    g_fw = rcopy(gd.at[o, mine], gd.at[o, mine], s_g, (2,), mate)
    g_ab = rcopy(gx_.at[mine], gx_.at[mine], s_g, (3,), mate)
    ab.s0()
    g_x.start()
    g_d2d.start()
    ab.s1()
    ab.s2()
    g_got.wait_recv()
    g_fw.start()
    ab.s3()
    g_d2d.wait_recv()
    g_fw.wait_recv()
    ab.s4()
    gh[0:256], gl[0:256] = split(gd[0])
    gh[256:512], gl[256:512] = split(gd[1])
    ab.s5()
    g_ab.start()
    g_ab.wait_recv()
    gh[512:768], gl[512:768] = split(gx_[...])

    pad = jnp.zeros((64, 512), F32)
    rr = lax.broadcasted_iota(jnp.int32, (64, 128), 0)
    cc = lax.broadcasted_iota(jnp.int32, (64, 128), 1)
    eye = jnp.where(cc == rr + 64, 1.0, 0.0).astype(F32)

    @pl.loop(0, ITERS)
    def _(step):
        bh, bl = split(bt[...])
        d0 = gh[0:256, :], gl[0:256, :]
        d1 = gh[256:512, :], gl[256:512, :]
        ax = gh[512:768, :], gl[512:768, :]
        ba = bh[:, 0:256], bl[:, 0:256]
        bb = bh[:, 256:512], bl[:, 256:512]
        left = dot3(*ba, *d0, NN) + dot3(*bb, *ax, NT)
        right = dot3(*ba, *ax, NN) + dot3(*bb, *d1, NN)
        block = jnp.concatenate([left, right], axis=1)
        small = lax.dot_general(
            block, jnp.concatenate([block, pad], axis=0), NT, precision=HI, preferred_element_type=F32
        )
        w = eliminate(small + eye)
        w = jnp.where(cc >= 64, w, 0.0)
        bt[...] = lax.dot_general(
            w, jnp.concatenate([pad, block], axis=0), NN, precision=HI, preferred_element_type=F32
        )

    hi, lo = split(bt[...])
    fh[...] = hi
    fl[...] = lo

    def ranks(g):
        return pl.ds(pl.multiple_of(g * 16, 16), 16)

    def c_core(v):
        return rcopy(psend.at[v], precv.at[v], s_c, (v,), across)

    ours, theirs = ranks(me), ranks(2 * o + c)

    @pl.loop(0, nv)
    def _(v):
        ah = jnp.concatenate([fh[theirs, :], fh[ours, :]], axis=0)
        al = jnp.concatenate([fl[theirs, :], fl[ours, :]], axis=0)
        res = dot3(ah, al, Xh[v], Xl[v], NN)
        psend[v] = res[0:16]
        c_core(v).start()
        for j in range(4):
            core_ref[pl.ds(v * 8 + 4 * h + j, 16, stride=8 * nv), :] = res[16:32, 128 * j : 128 * j + 128]

    for g in range(4):
        factor_ref[125 * g : 125 * g + 125, :] = bt[:, 128 * g : 128 * g + 128].T[0:125, :]

    @pl.loop(0, nv)
    def _(v):
        c_core(v).wait_recv()
        got = precv[v]
        for j in range(4):
            core_ref[pl.ds(v * 8 + 4 * o + j, 16, stride=8 * nv), :] = got[:, 128 * j : 128 * j + 128]

    @pl.loop(0, nv)
    def _(v):
        c_x(v).wait_send()
        c_d2d(v).wait_send()
        c_fw(v).wait_send()
        c_core(v).wait_send()

    own.finish()
    ab.finish()
    for g in (g_d2d, g_x, g_fw, g_ab):
        g.wait_send()


def per_device(nz, ny, fields, var_scale, start_basis):
    nv = fields.shape[0]
    x = fields.reshape(nv, 125, 2, 4, 128)
    rz = 128 // nz
    ry = rz // ny
    block = (128, 4, 128)
    reduce_bufs = lambda slots: [
        pltpu.VMEM((max(nz - 1, 1), rz, 256), F32),
        pltpu.VMEM((rz, 256), F32),
        pltpu.VMEM((max(ny - 1, 1), ry, 256), F32),
        pltpu.VMEM((ry, 256), F32),
        pltpu.VMEM((slots, ry, 256), F32),
    ]
    dma = pltpu.SemaphoreType.DMA
    factor, core = pl.pallas_call(
        functools.partial(kernel, nv, nz, ny),
        out_shape=(
            jax.ShapeDtypeStruct((500, 64), F32),
            jax.ShapeDtypeStruct((16 * nv * 8, 128), F32),
        ),
        in_specs=[
            pl.BlockSpec(memory_space=pltpu.SMEM),
            pl.BlockSpec(memory_space=pl.ANY),
            pl.BlockSpec(memory_space=pltpu.VMEM),
        ],
        out_specs=(pl.BlockSpec(memory_space=pltpu.VMEM), pl.BlockSpec(memory_space=pltpu.VMEM)),
        scratch_shapes=[
            pltpu.VMEM((nv, 2) + block, F32),
            pltpu.VMEM((nv, 2) + block, F32),
            pltpu.VMEM((nv,) + block, F32),
            pltpu.VMEM((nv,) + block, F32),
            pltpu.VMEM((nv, 512, 512), BF16),
            pltpu.VMEM((nv, 512, 512), BF16),
            pltpu.VMEM((256, 512), BF16),
            pltpu.VMEM((256, 512), BF16),
            pltpu.VMEM((128, 256), F32),
            pltpu.VMEM((128, 256), F32),
            *reduce_bufs(2),
            *reduce_bufs(4),
            pltpu.VMEM((2, 256, 256), F32),
            pltpu.VMEM((256, 256), F32),
            pltpu.VMEM((768, 256), BF16),
            pltpu.VMEM((768, 256), BF16),
            pltpu.VMEM((64, 512), F32),
            pltpu.VMEM((64, 512), BF16),
            pltpu.VMEM((64, 512), BF16),
            pltpu.VMEM((nv, 16, 512), F32),
            pltpu.VMEM((nv, 16, 512), F32),
            dma((nv, 2)),
            dma((2, nv)),
            dma((2, nv)),
            dma((2, nv)),
            dma((2, 5, 3)),
            dma((2, 5, 3)),
            dma((2, 4)),
            dma((2, nv)),
        ],
        compiler_params=pltpu.CompilerParams(
            collective_id=0, has_side_effects=True, vmem_limit_bytes=60 * 1024 * 1024
        ),
        name="tucker",
    )(var_scale, x, start_basis)
    return factor, core.reshape(16, nv, 8, 128)


def solution(mesh):
    nz = mesh.shape["gy"]
    ny = mesh.shape["gz"] // 2
    in_specs = (P(None, "gx", "gy", "gz"), P(), P())
    out_specs = (P(), P("gx", None, "gy", "gz"))
    return jax.shard_map(
        functools.partial(per_device, nz, ny), mesh=mesh, in_specs=in_specs, out_specs=out_specs, check_vma=False
    )
```

time: 326 us -> 126 us (0.39)
  waiting for transfers between devices: 151 us -> 0 us
  Pallas kernels: 0 us -> 120 us
  blocking collectives: 80.3 us -> 0 us
  other arithmetic: 39.3 us -> 0 us
  matrix products: 28.4 us -> 0 us
  between operations: 14.2 us -> 0.64 us
  local copies, waits for them, and re-layouts: 12.1 us -> 5.47 us
    psum x1 -> x0, waiting for transfers between devices: 151 us -> none  [per_device(): gram = lax.psum(partial_gram, ('gx', 'gy', 'gz'))]
    pallas_call x0 -> x1, Pallas kernels: none -> 120 us  [per_device(): pl.pallas_call(functools.partial(kernel, nv, nz, ny), out_shape=(jax.Shap...]
    all_to_all x2 -> x0, blocking collectives: 80.3 us -> none  [the longest x1 68 us: per_device(): lax.all_to_all(scaled, 'gx', split_axis=2, concat_axis=1, tiled=True)]
    another operation x15 -> x0, other arithmetic: 36.2 us -> none  [the longest x9 19.6 us: orthonormal(): lower = jnp.linalg.cholesky(small)]
    dot_general x8 -> x0, matrix products: 27.4 us -> none  [the longest x1 13.6 us: per_device(): lax.dot_general(swapped, swapped, contract, precision=lax.Precision.HIGHEST)]
    all_to_all x3 -> x0, local copies, waits for them, and re-layouts: 10.2 us -> none  [the longest x2 9.05 us: per_device(): lax.all_to_all(scaled, 'gx', split_axis=2, concat_axis=1, tiled=True)]
    unnamed x4 -> x3, local copies, waits for them, and re-layouts: 0.02 us -> 5.47 us
  transfers between devices with their start and end apart: 1 -> 0, of which waited for: 1 -> 0; matrix products, arithmetic and copies ran while one was open for 0% -> 0% of each run, Pallas kernels for 0% -> 0%
where the time goes in v1:
time: 126 us
  Pallas kernels  120 us (95%)
  local copies, waits for them, and re-layouts  5.47 us (4%)
    pallas_call x1, Pallas kernels, per_device(): pl.pallas_call(functools.partial(kernel, nv, nz, ny), out_shape=(jax.Shap...  120 us
    unnamed x3, local copies, waits for them, and re-layouts  5.47 us

profile of v1, /device:TPU:1, one launch (start us, length us, event | category | flops | bytes accessed | tf_op | source)
XLA Modules:
  0.0 125.7 jit_solution(14270037833241215867)
XLA Ops:
  0.6 1.7 %copy.5.start_ref = f32[500,64]{1,0:T(8,128)} copy(f32[500,64]{0,1:T(8,128)} %param.5) | data formatting | bytes 256000 | tf_op args[2]
  2.4 119.6 %tucker.1 = (f32[500,64]{1,0:T(8,128)}, f32[1408,128]{1,0:T(8,128)}) custom-call(f32[11]{0:T(128)} %scale_ref.1, f32[11,125,2,4,128]{4,3,2,1,0:T(4,128)} %bitcast.2, f32[500,64]{1,0:T(8,128)} %copy.5.start_ref), custom_call_target="tpu_custom_call" | custom-call | tf_op jit(solution)/shard_map/tucker/pallas_call | solution.py:378
  122.0 1.7 %copy.6 = f32[500,64]{0,1:T(8,128)} copy(f32[500,64]{1,0:T(8,128)} %get-tuple-element.6) | data formatting | bytes 256000
  123.7 2.0 %copy.8 = f32[16,11,8,128]{3,2,1,0:T(8,128)} copy(f32[16,11,8,128]{3,2,1,0:T(8,128)} %bitcast.3) | data formatting | bytes 1441792

commit v2 on v1

--- a/solution.py
+++ b/solution.py
@@ -66,7 +66,7 @@
     factor_ref, core_ref,
     xo, xd, xx, xf, Xh, Xl, Yh, Yl,
     acc_own, acc_ab,
-    zb_o, b1_o, yb_o, b2_o, xb_o, zb_a, b1_a, yb_a, b2_a, xb_a,
+    pb_o, b2_o, xb_o, pb_a, b2_a, xb_a,
     gd, gx_, gh, gl, bt, fh, fl, psend, precv,
     s_loc, s_d2d, s_x, s_fw, s_ro, s_ra, s_g, s_c,
 ):
@@ -78,16 +78,21 @@
     o = 1 - h
     xh = hy // ny
     y = lax.rem(hy, ny)
-    rz = 128 // nz
-    ry = rz // ny
+    ry = 128 // (nz * ny)
 
     def dev(gx=me, gy=z, xhi=xh, yy=y):
         return {"gx": gx, "gy": gy, "gz": xhi * ny + yy}
 
     mate = dev(gx=2 * h + (1 - c))
     across = dev(gx=2 * o + c)
-    zs = [dev(gy=lax.rem(z + d, nz)) for d in range(1, nz)]
-    ys = [dev(yy=lax.rem(y + d, ny)) for d in range(1, ny)]
+    np_ = nz * ny - 1
+    spot = z * ny + y
+    plane = []
+    for dz in range(nz):
+        for dy in range(ny):
+            if dz or dy:
+                tz, ty = lax.rem(z + dz, nz), lax.rem(y + dy, ny)
+                plane.append((dz * ny + dy, tz * ny + ty, dev(gy=tz, yy=ty)))
     x_hi = dev(xhi=1 - xh)
     x_all = [x_hi, across, dev(gx=2 * o + c, xhi=1 - xh)]
 
@@ -114,7 +119,7 @@
         local(v, h).start()
 
     barrier = pltpu.get_barrier_semaphore()
-    greet = [mate] + zs + ys + x_all
+    greet = [mate] + [d for _, _, d in plane] + x_all
     for d in greet:
         pl.semaphore_signal(barrier, inc=1, device_id=d, device_id_type=MESH)
     zero = jnp.zeros((3, 4, 128), F32)
@@ -126,19 +131,24 @@
         xf[v, 125:128] = zero
     pl.semaphore_wait(barrier, len(greet))
 
+    ahead = min(4, nv)
+
     @pl.loop(0, nv)
     def _(v):
         local(v, o).wait()
-        c_x(v).start()
+
+        @pl.when(v < ahead)
+        def _():
+            c_x(v).start()
+
         local(v, h).wait()
         c_d2d(v).start()
 
     acc_own[...] = jnp.zeros_like(acc_own)
     acc_ab[...] = jnp.zeros_like(acc_ab)
-    zrow = jnp.zeros((3, 64), F32)
+    bt[...] = jnp.zeros_like(bt)
     for g in range(4):
-        part = jnp.concatenate([start_ref[125 * g : 125 * g + 125, :], zrow], axis=0)
-        bt[:, 128 * g : 128 * g + 128] = part.T
+        bt[:, 128 * g : 128 * g + 125] = start_ref[:, 125 * g : 125 * g + 125]
 
     def convert(block, s, dh, dl):
         for j in range(4):
@@ -164,97 +174,87 @@
         ) + dot3(Yh[rows(c), :], Yl[rows(c), :], Yh[...], Yl[...], NT)
 
     class Reduce:
-        def __init__(self, acc, zb, b1, yb, b2, xb, out, sems, partners, slot, slots):
-            self.acc, self.zb, self.b1, self.yb, self.b2, self.xb = acc, zb, b1, yb, b2, xb
+        def __init__(self, acc, pb, b2, xb, out, sems, partners, slot, slots):
+            self.acc, self.pb, self.b2, self.xb = acc, pb, b2, xb
             self.out, self.sems, self.partners, self.slot, self.slots = out, sems, partners, slot, slots
 
-        def at(self, n, start):
-            return pl.ds(pl.multiple_of(start, ry), n)
-
-        def zc(self, d):
-            to = lax.rem(z + d, nz)
-            return rcopy(self.acc.at[self.at(rz, to * rz)], self.zb.at[d - 1], self.sems, (0, d - 1), zs[d - 1])
-
-        def yc(self, d):
-            to = lax.rem(y + d, ny)
-            return rcopy(self.b1.at[self.at(ry, to * ry)], self.yb.at[d - 1], self.sems, (1, d - 1), ys[d - 1])
+        def piece(self, start):
+            return pl.ds(pl.multiple_of(start, ry), ry)
+
+        def rs(self, k):
+            _, to, d = plane[k]
+            return rcopy(self.acc.at[self.piece(to * ry)], self.pb.at[k], self.sems, (k,), d)
 
         def xc(self, k):
-            return rcopy(self.b2, self.xb.at[self.slot], self.sems, (2, k), self.partners[k])
-
-        def yg(self, d):
-            here = self.out.at[self.at(ry, c * 128 + z * rz + y * ry)]
-            return rcopy(here, here, self.sems, (3, d - 1), ys[d - 1])
-
-        def zg(self, d):
-            here = self.out.at[self.at(rz, c * 128 + z * rz)]
-            return rcopy(here, here, self.sems, (4, d - 1), zs[d - 1])
+            return rcopy(self.b2, self.xb.at[self.slot], self.sems, (2 * np_ + k,), self.partners[k])
+
+        def ag(self, k):
+            here = self.out.at[self.piece(c * 128 + spot * ry)]
+            return rcopy(here, here, self.sems, (np_ + k,), plane[k][2])
 
         def s0(self):
-            for d in range(1, nz):
-                self.zc(d).start()
+            for k in range(np_):
+                self.rs(k).start()
 
         def s1(self):
-            for d in range(1, nz):
-                self.zc(d).wait_recv()
-            t = self.acc[self.at(rz, z * rz), :]
-            for d in range(1, nz):
-                t = t + self.zb[d - 1]
-            self.b1[...] = t
-            for d in range(1, ny):
-                self.yc(d).start()
-
-        def s2(self):
-            for d in range(1, ny):
-                self.yc(d).wait_recv()
-            t = self.b1[self.at(ry, y * ry), :]
-            for d in range(1, ny):
-                t = t + self.yb[d - 1]
+            for k in range(np_):
+                self.rs(k).wait_recv()
+            t = self.acc[self.piece(spot * ry), :]
+            for k in range(np_):
+                t = t + self.pb[k]
             self.b2[...] = t
             for k in range(len(self.partners)):
                 self.xc(k).start()
             self.xb[self.slot] = t
 
-        def s3(self):
+        def s2(self):
             for k in range(len(self.partners)):
                 self.xc(k).wait_recv()
             t = self.xb[0]
             for k in range(1, self.slots):
                 t = t + self.xb[k]
-            self.out[self.at(ry, c * 128 + z * rz + y * ry), :] = t
-            for d in range(1, ny):
-                self.yg(d).start()
-
-        def s4(self):
-            for d in range(1, ny):
-                self.yg(d).wait_recv()
-            for d in range(1, nz):
-                self.zg(d).start()
-
-        def s5(self):
-            for d in range(1, nz):
-                self.zg(d).wait_recv()
+            self.out[self.piece(c * 128 + spot * ry), :] = t
+            for k in range(np_):
+                self.ag(k).start()
+
+        def s3(self):
+            for k in range(np_):
+                self.ag(k).wait_recv()
 
         def finish(self):
-            for d in range(1, nz):
-                self.zc(d).wait_send()
-                self.zg(d).wait_send()
-            for d in range(1, ny):
-                self.yc(d).wait_send()
-                self.yg(d).wait_send()
+            for k in range(np_):
+                self.rs(k).wait_send()
+                self.ag(k).wait_send()
             for k in range(len(self.partners)):
                 self.xc(k).wait_send()
 
-    own = Reduce(acc_own, zb_o, b1_o, yb_o, b2_o, xb_o, gd.at[h], s_ro, [x_hi], xh, 2)
-    ab = Reduce(acc_ab, zb_a, b1_a, yb_a, b2_a, xb_a, gx_, s_ra, x_all, xh * 2 + h, 4)
+    own = Reduce(acc_own, pb_o, b2_o, xb_o, gd.at[h], s_ro, [x_hi], xh, 2)
+    ab = Reduce(acc_ab, pb_a, b2_a, xb_a, gx_, s_ra, x_all, xh * 2 + h, 4)
+
+    mine = pl.ds(pl.multiple_of(c * 128, 128), 128)
+    g_d2d = rcopy(gd.at[h, mine], gd.at[h, mine], s_g, (0,), mate)
+    g_x = rcopy(gd.at[h, mine], gd.at[h, mine], s_g, (1,), across)
+    g_got = rcopy(gd.at[o, mine], gd.at[o, mine], s_g, (1,), across)
+    g_fw = rcopy(gd.at[o, mine], gd.at[o, mine], s_g, (2,), mate)
+    g_ab = rcopy(gx_.at[mine], gx_.at[mine], s_g, (3,), mate)
+
+    def own_done():
+        own.s3()
+        g_x.start()
+        g_d2d.start()
 
     own.s0()
-    steps = {1: own.s1, 3: own.s2, 5: own.s3, 7: own.s4, 9: own.s5}
+    steps = {1: own.s1, 8: own.s2, 10: own_done}
 
     @pl.loop(0, nv)
     def _(v):
         s = scale_ref[v]
         c_x(v).wait_recv()
+
+        @pl.when(v + ahead < nv)
+        def _():
+            c_x(v + ahead).start()
+
         c_fw(v).start()
         g2 = 2 * o + c
         convert(xx.at[v], s, Xh.at[v, rows(g2)], Xl.at[v, rows(g2)])
@@ -267,26 +267,16 @@
             Xh[v, rows(c), :], Xl[v, rows(c), :], Xh[v, 256:512, :], Xl[v, 256:512, :], NT
         )
 
-    mine = pl.ds(pl.multiple_of(c * 128, 128), 128)
-    g_d2d = rcopy(gd.at[h, mine], gd.at[h, mine], s_g, (0,), mate)
-    g_x = rcopy(gd.at[h, mine], gd.at[h, mine], s_g, (1,), across)
-    g_got = rcopy(gd.at[o, mine], gd.at[o, mine], s_g, (1,), across)
-    g_fw = rcopy(gd.at[o, mine], gd.at[o, mine], s_g, (2,), mate)
-    g_ab = rcopy(gx_.at[mine], gx_.at[mine], s_g, (3,), mate)
     ab.s0()
-    g_x.start()
-    g_d2d.start()
     ab.s1()
-    ab.s2()
     g_got.wait_recv()
     g_fw.start()
-    ab.s3()
+    ab.s2()
     g_d2d.wait_recv()
     g_fw.wait_recv()
-    ab.s4()
     gh[0:256], gl[0:256] = split(gd[0])
     gh[256:512], gl[256:512] = split(gd[1])
-    ab.s5()
+    ab.s3()
     g_ab.start()
     g_ab.wait_recv()
     gh[512:768], gl[512:768] = split(gx_[...])
@@ -339,7 +329,7 @@
             core_ref[pl.ds(v * 8 + 4 * h + j, 16, stride=8 * nv), :] = res[16:32, 128 * j : 128 * j + 128]
 
     for g in range(4):
-        factor_ref[125 * g : 125 * g + 125, :] = bt[:, 128 * g : 128 * g + 128].T[0:125, :]
+        factor_ref[:, 125 * g : 125 * g + 125] = bt[:, 128 * g : 128 * g + 125]
 
     @pl.loop(0, nv)
     def _(v):
@@ -364,13 +354,11 @@
 def per_device(nz, ny, fields, var_scale, start_basis):
     nv = fields.shape[0]
     x = fields.reshape(nv, 125, 2, 4, 128)
-    rz = 128 // nz
-    ry = rz // ny
+    ry = 128 // (nz * ny)
+    np_ = nz * ny - 1
     block = (128, 4, 128)
     reduce_bufs = lambda slots: [
-        pltpu.VMEM((max(nz - 1, 1), rz, 256), F32),
-        pltpu.VMEM((rz, 256), F32),
-        pltpu.VMEM((max(ny - 1, 1), ry, 256), F32),
+        pltpu.VMEM((np_, ry, 256), F32),
         pltpu.VMEM((ry, 256), F32),
         pltpu.VMEM((slots, ry, 256), F32),
     ]
@@ -378,7 +366,7 @@
     factor, core = pl.pallas_call(
         functools.partial(kernel, nv, nz, ny),
         out_shape=(
-            jax.ShapeDtypeStruct((500, 64), F32),
+            jax.ShapeDtypeStruct((64, 500), F32),
             jax.ShapeDtypeStruct((16 * nv * 8, 128), F32),
         ),
         in_specs=[
@@ -413,8 +401,8 @@
             dma((2, nv)),
             dma((2, nv)),
             dma((2, nv)),
-            dma((2, 5, 3)),
-            dma((2, 5, 3)),
+            dma((2, 2 * np_ + 3)),
+            dma((2, 2 * np_ + 3)),
             dma((2, 4)),
             dma((2, nv)),
         ],
@@ -422,8 +410,8 @@
             collective_id=0, has_side_effects=True, vmem_limit_bytes=60 * 1024 * 1024
         ),
         name="tucker",
-    )(var_scale, x, start_basis)
-    return factor, core.reshape(16, nv, 8, 128)
+    )(var_scale, x, start_basis.T)
+    return factor.T, core.reshape(16, nv, 8, 128)
 
 
 def solution(mesh):

time: 126 us -> 112 us (0.89)
  Pallas kernels: 120 us -> 108 us
  local copies, waits for them, and re-layouts: 5.47 us -> 3.58 us
    pallas_call x1, Pallas kernels: 120 us -> 108 us  [per_device(): pl.pallas_call(functools.partial(kernel, nv, nz, ny), out_shape=(jax.Shap...]
    unnamed x3 -> x2, local copies, waits for them, and re-layouts: 5.47 us -> 3.58 us
where the time goes in v2:
time: 112 us
  Pallas kernels  108 us (96%)
  local copies, waits for them, and re-layouts  3.58 us (3%)
    pallas_call x1, Pallas kernels, per_device(): pl.pallas_call(functools.partial(kernel, nv, nz, ny), out_shape=(jax.Shap...  108 us
    unnamed x2, local copies, waits for them, and re-layouts  3.58 us

profile of v2, /device:TPU:1, one launch (start us, length us, event | category | flops | bytes accessed | tf_op | source)
XLA Modules:
  0.0 112.0 jit_solution(10045921728835022410)
XLA Ops:
  0.6 107.7 %tucker.1 = (f32[64,500]{1,0:T(8,128)}, f32[1408,128]{1,0:T(8,128)}) custom-call(f32[11]{0:T(128)} %scale_ref.1, f32[11,125,2,4,128]{4,3,2,1,0:T(4,128)} %bitcast.4, f32[64,500]{1,0:T(8,128)} %bitcast.6), custom_call_target="tpu_custom_call" | custom-call | tf_op jit(solution)/shard_map/tucker/pallas_call | solution.py:366
  108.4 1.6 %copy.7 = f32[500,64]{0,1:T(8,128)} copy(f32[500,64]{0,1:T(8,128)} %bitcast.7) | data formatting | bytes 256000
  109.9 2.0 %copy.8 = f32[16,11,8,128]{3,2,1,0:T(8,128)} copy(f32[16,11,8,128]{3,2,1,0:T(8,128)} %bitcast.5) | data formatting | bytes 1441792

commit v3 on v2

v3 whole, which is shorter than its diff:
```python
import functools

import jax
import jax.numpy as jnp
from jax import lax
from jax.experimental import pallas as pl
from jax.experimental.pallas import tpu as pltpu
from jax.sharding import PartitionSpec as P

ITERS = 3
MESH = pl.DeviceIdType.MESH
NN = (((1,), (0,)), ((), ()))
NT = (((1,), (1,)), ((), ()))
F32 = jnp.float32
BF16 = jnp.bfloat16
HI = lax.Precision.HIGHEST


def split(x):
    hi = x.astype(BF16)
    return hi, (x - hi.astype(F32)).astype(BF16)


def dot(a, b, dims):
    return lax.dot_general(a, b, dims, preferred_element_type=F32)


def dot3(ah, al, bh, bl, dims):
    return dot(ah, bh, dims) + (dot(ah, bl, dims) + dot(al, bh, dims))


def column(block, j):
    return block.reshape(512, 128)[pl.ds(j, 128, stride=4), :]


def eliminate(m):
    tiles = [m[8 * t : 8 * t + 8, :] for t in range(8)]
    sub = lax.broadcasted_iota(jnp.int32, (8, 128), 0)

    def spread_row(tile, k):
        return jnp.broadcast_to(tile[k : k + 1, :], (8, 128))

    for first in range(0, 64, 16):
        top = first // 8
        cols = [
            {t: jnp.broadcast_to(tiles[t][:, first + k : first + k + 1], (8, 128)) for t in range(top, 8)}
            for k in range(16)
        ]
        for k in range(16):
            q, r = top + k // 8, k % 8
            if r == 0:
                pivots = jnp.ones((8, 128), F32)
            p = spread_row(cols[k][q], r)
            rp = 1.0 / p
            row = spread_row(tiles[q], r)
            across = {l: spread_row(cols[l][q], r) for l in range(k + 1, 16)}
            for t in range(q, 8):
                f = cols[k][t] * rp
                if t == q:
                    f = jnp.where(sub > r, f, 0.0)
                tiles[t] = tiles[t] - f * row
                for l in range(k + 1, 16):
                    cols[l][t] = cols[l][t] - f * across[l]
            pivots = jnp.where(sub == r, p, pivots)
            if r == 7:
                y = lax.rsqrt(pivots)
                tiles[q] = tiles[q] * (y * (1.5 - 0.5 * (pivots * y) * y))
    return jnp.concatenate(tiles, axis=0)


def kernel(
    nv, ne, nz, ny, scale_ref, x_ref, start_ref,
    factor_ref, core_ref,
    xo, xd, xx, xf, xe, xg, Xh, Xl, Yh, Yl,
    acc_own, acc_ab,
    pb_o, b2_o, xb_o, pb_a, b2_a, xb_a,
    gd, gk, gm, gh, gl, bt, fh, fl, psend, precv,
    s_loc, s_d2d, s_x, s_fw, s_e, s_ef, s_ro, s_ra, s_g, s_c,
):
    me = lax.axis_index("gx")
    z = lax.axis_index("gy")
    hy = lax.axis_index("gz")
    h = me // 2
    c = lax.rem(me, 2)
    o = 1 - h
    xh = hy // ny
    y = lax.rem(hy, ny)
    ry = 128 // (nz * ny)

    def dev(gx=me, gy=z, xhi=xh, yy=y):
        return {"gx": gx, "gy": gy, "gz": xhi * ny + yy}

    mate = dev(gx=2 * h + (1 - c))
    across = dev(gx=2 * o + c)
    np_ = nz * ny - 1
    spot = z * ny + y
    plane = []
    for dz in range(nz):
        for dy in range(ny):
            if dz or dy:
                tz, ty = lax.rem(z + dz, nz), lax.rem(y + dy, ny)
                plane.append((dz * ny + dy, tz * ny + ty, dev(gy=tz, yy=ty)))
    x_hi = dev(xhi=1 - xh)
    x_all = [x_hi, across, dev(gx=2 * o + c, xhi=1 - xh)]
    x_cross = [dev(gx=2 * o + (1 - c)), dev(gx=2 * o + (1 - c), xhi=1 - xh)]

    def rcopy(src, dst, sems, at, to):
        return pltpu.make_async_remote_copy(
            src_ref=src, dst_ref=dst, send_sem=sems.at[(0,) + at], recv_sem=sems.at[(1,) + at],
            device_id=to, device_id_type=MESH,
        )

    def local(v, half):
        return pltpu.make_async_copy(x_ref.at[v, :, half], xo.at[v, half, 0:125], s_loc.at[v, half])

    def c_d2d(v):
        return rcopy(xo.at[v, :, 0:125], xd.at[v, :, 0:125], s_d2d, (v,), mate)

    def c_x(v):
        return rcopy(xo.at[v, o, 0:125], xx.at[v, 0:125], s_x, (v,), across)

    def c_fw(v):
        return rcopy(xx.at[v, 0:125], xf.at[v, 0:125], s_fw, (v,), mate)

    def c_e(v):
        return rcopy(xo.at[v, h, 0:125], xe.at[v, 0:125], s_e, (v,), across)

    def c_ef(v):
        return rcopy(xe.at[v, 0:125], xg.at[v, 0:125], s_ef, (v,), mate)

    for v in range(nv):
        local(v, o).start()
        local(v, h).start()

    barrier = pltpu.get_barrier_semaphore()
    greet = [mate] + [d for _, _, d in plane] + x_all + x_cross
    for d in greet:
        pl.semaphore_signal(barrier, inc=1, device_id=d, device_id_type=MESH)
    zero = jnp.zeros((3, 4, 128), F32)
    for v in range(nv):
        for half in range(2):
            xo[v, half, 125:128] = zero
            xd[v, half, 125:128] = zero
        xx[v, 125:128] = zero
        xf[v, 125:128] = zero
    for v in range(ne):
        xe[v, 125:128] = zero
        xg[v, 125:128] = zero
    pl.semaphore_wait(barrier, len(greet))

    ahead = min(4, nv)

    @pl.loop(0, nv)
    def _(v):
        local(v, o).wait()

        @pl.when(v < ahead)
        def _():
            c_x(v).start()

        local(v, h).wait()
        c_d2d(v).start()

    acc_own[...] = jnp.zeros_like(acc_own)
    acc_ab[...] = jnp.zeros_like(acc_ab)
    bt[...] = jnp.zeros_like(bt)
    for g in range(4):
        bt[:, 128 * g : 128 * g + 125] = start_ref[:, 125 * g : 125 * g + 125]

    def convert(block, s, dh, dl):
        for j in range(4):
            hi, lo = split(column(block, j) * s)
            dh[:, 128 * j : 128 * j + 128] = hi
            dl[:, 128 * j : 128 * j + 128] = lo

    def rows(g, n=128):
        return pl.ds(pl.multiple_of(g * 128, 128), n)

    @pl.loop(0, nv)
    def _(v):
        s = scale_ref[v]
        w = jnp.minimum(v, ne)
        convert(xo.at[v, h], s, Xh.at[v, rows(me)], Xl.at[v, rows(me)])
        convert(xo.at[v, o], s, Yh.at[w, rows(me)], Yl.at[w, rows(me)])
        c_d2d(v).wait_recv()
        m2 = 2 * h + (1 - c)
        convert(xd.at[v, h], s, Xh.at[v, rows(m2)], Xl.at[v, rows(m2)])
        convert(xd.at[v, o], s, Yh.at[w, rows(m2)], Yl.at[w, rows(m2)])
        chip = pl.ds(pl.multiple_of(h * 256, 256), 256)
        acc_own[...] += dot3(
            Xh[v, rows(me), :], Xl[v, rows(me), :], Xh[v, chip, :], Xl[v, chip, :], NT
        ) + dot3(Yh[w, rows(me), :], Yl[w, rows(me), :], Yh[w, chip, :], Yl[w, chip, :], NT)

    def piece(base, p):
        return pl.ds(pl.multiple_of(base + p * ry, ry), ry)

    my_rows = piece(c * 128, spot)
    mine = pl.ds(pl.multiple_of(c * 128, 128), 128)

    def o_rs(k):
        _, to, d = plane[k]
        return rcopy(acc_own.at[piece(0, to)], pb_o.at[k], s_ro, (k,), d)

    def o_x(k):
        return rcopy(b2_o, xb_o.at[xh, h], s_ro, (2 * np_ + k,), x_all[k])

    def o_ag(k):
        return rcopy(gd.at[:, my_rows], gd.at[:, my_rows], s_ro, (np_ + k,), plane[k][2])

    g_own = rcopy(gd.at[:, mine], gd.at[:, mine], s_g, (0,), mate)

    def own_1():
        for k in range(np_):
            o_rs(k).wait_recv()
        t = acc_own[piece(0, spot), :]
        for k in range(np_):
            t = t + pb_o[k]
        b2_o[...] = t
        for k in range(3):
            o_x(k).start()
        xb_o[xh, h] = t

    def own_2():
        for k in range(3):
            o_x(k).wait_recv()
        for side in range(2):
            gd[side, my_rows, :] = xb_o[0, side] + xb_o[1, side]
        for k in range(np_):
            o_ag(k).start()

    def own_3():
        for k in range(np_):
            o_ag(k).wait_recv()
        g_own.start()

    def a_rs(k):
        _, to, d = plane[k]
        return rcopy(acc_ab.at[:, piece(0, to)], pb_a.at[k], s_ra, (k,), d)

    def a_x(k):
        at = (2 * np_ + k,)
        if k == 0:
            return rcopy(b2_a, xb_a.at[xh, h], s_ra, at, x_hi)
        if k < 3:
            return rcopy(b2_a.at[c], xb_a.at[xh, h, c], s_ra, at, x_all[k])
        return rcopy(b2_a.at[1 - c], xb_a.at[xh, h, c], s_ra, at, x_cross[k - 3])

    def a_ag(k):
        here = gk.at[:, piece(0, spot)]
        return rcopy(here, here, s_ra, (np_ + k,), plane[k][2])

    g_ab = rcopy(gk, gm, s_g, (1,), mate)

    for k in range(np_):
        o_rs(k).start()
    steps = {1: own_1, 7: own_2, 9: own_3}
    g2 = 2 * o + c
    g3 = 2 * o + (1 - c)

    def late(v):
        c_fw(v).wait_recv()
        convert(xf.at[v], scale_ref[v], Xh.at[v, rows(g3)], Xl.at[v, rows(g3)])

    @pl.loop(0, nv)
    def _(v):
        c_x(v).wait_recv()

        @pl.when(v + ahead < nv)
        def _():
            c_x(v + ahead).start()

        c_fw(v).start()
        convert(xx.at[v], scale_ref[v], Xh.at[v, rows(g2)], Xl.at[v, rows(g2)])
        for k, f in steps.items():
            pl.when(v == k * nv // 11)(f)
        for k in range(2):
            left = rows(g2 + (1 - h) * (2 * h + k - g2))
            right = rows(g2 + h * (2 * h + k - g2))
            acc_ab[k] += dot3(Xh[v, left, :], Xl[v, left, :], Xh[v, right, :], Xl[v, right, :], NT)

        @pl.when((v > 0) & (v < nv - 1))
        def _():
            late(v - 1)

    for k in range(np_):
        a_rs(k).start()
    c_e(0).start()
    late(nv - 2)
    late(nv - 1)
    g_own.wait_recv()
    gh[0:256], gl[0:256] = split(gd[0])
    gh[256:512], gl[256:512] = split(gd[1])
    for k in range(np_):
        a_rs(k).wait_recv()
    t = acc_ab[:, piece(0, spot), :]
    for k in range(np_):
        t = t + pb_a[k]
    b2_a[...] = t
    for k in range(5):
        a_x(k).start()
    xb_a[xh, h] = t
    for v in range(1, ne):
        c_e(v).start()
    for k in range(3):
        a_x(k).wait_recv()
    for k in range(3, 5):
        rcopy(b2_a.at[1 - c], xb_a.at[xh, o, 1 - c], s_ra, (2 * np_ + k,), x_cross[k - 3]).wait_recv()
    gk[:, piece(0, spot), :] = (xb_a[0, 0] + xb_a[0, 1]) + (xb_a[1, 0] + xb_a[1, 1])
    for k in range(np_):
        a_ag(k).start()
    c_e(0).wait_recv()
    c_ef(0).start()
    for k in range(np_):
        a_ag(k).wait_recv()
    g_ab.start()

    def spread(ref, core):
        for k in range(2):
            hi, lo = split(ref[k])
            at = pl.ds(pl.multiple_of(512 + 128 * (core + (1 - h) * (k - core)), 128), 128)
            to = pl.ds(pl.multiple_of(128 * (core + h * (k - core)), 128), 128)
            gh[at, to] = hi
            gl[at, to] = lo

    spread(gk, c)
    g_ab.wait_recv()
    spread(gm, 1 - c)

    pad = jnp.zeros((64, 512), F32)
    rr = lax.broadcasted_iota(jnp.int32, (64, 128), 0)
    cc = lax.broadcasted_iota(jnp.int32, (64, 128), 1)
    eye = jnp.where(cc == rr + 64, 1.0, 0.0).astype(F32)

    def times_gram(b):
        bh, bl = split(b)
        d0 = gh[0:256, :], gl[0:256, :]
        d1 = gh[256:512, :], gl[256:512, :]
        ax = gh[512:768, :], gl[512:768, :]
        ba = bh[:, 0:256], bl[:, 0:256]
        bb = bh[:, 256:512], bl[:, 256:512]
        left = dot3(*ba, *d0, NN) + dot3(*bb, *ax, NT)
        right = dot3(*ba, *ax, NN) + dot3(*bb, *d1, NN)
        return jnp.concatenate([left, right], axis=1)

    block = times_gram(bt[...])
    for step in range(ITERS):
        small = lax.dot_general(
            block, jnp.concatenate([block, pad], axis=0), NT, precision=HI, preferred_element_type=F32
        )
        after = times_gram(block) if step < ITERS - 1 else block
        w = eliminate(small + eye)
        w = jnp.where(cc >= 64, w, 0.0)
        block = dot3(*split(w), *split(jnp.concatenate([pad, after], axis=0)), NN)
        if 1 <= step < ne:
            c_e(step).wait_recv()
            c_ef(step).start()
    bt[...] = block

    hi, lo = split(bt[...])
    fh[...] = hi
    fl[...] = lo

    def ranks(g):
        return pl.ds(pl.multiple_of(g * 16, 16), 16)

    def c_core(v):
        return rcopy(psend.at[v], precv.at[v], s_c, (v,), across)

    ours, theirs = ranks(me), ranks(2 * o + c)

    def put(v, half, val):
        for j in range(4):
            core_ref[pl.ds(v * 8 + 4 * half + j, 16, stride=8 * nv), :] = val[:, 128 * j : 128 * j + 128]

    @pl.loop(ne, nv)
    def _(v):
        ah = jnp.concatenate([fh[theirs, :], fh[ours, :]], axis=0)
        al = jnp.concatenate([fl[theirs, :], fl[ours, :]], axis=0)
        res = dot3(ah, al, Xh[v], Xl[v], NN)
        psend[v] = res[0:16]
        c_core(v).start()
        put(v, h, res[16:32])

    for g in range(4):
        factor_ref[:, 125 * g : 125 * g + 125] = bt[:, 128 * g : 128 * g + 125]

    for v in range(ITERS, ne):
        c_e(v).wait_recv()
        c_ef(v).start()

    @pl.loop(0, ne)
    def _(v):
        put(v, h, dot3(fh[ours, :], fl[ours, :], Xh[v], Xl[v], NN))
        s = scale_ref[v]
        convert(xe.at[v], s, Yh.at[v, rows(g2)], Yl.at[v, rows(g2)])
        c_ef(v).wait_recv()
        convert(xg.at[v], s, Yh.at[v, rows(g3)], Yl.at[v, rows(g3)])
        put(v, o, dot3(fh[ours, :], fl[ours, :], Yh[v], Yl[v], NN))

    @pl.loop(ne, nv)
    def _(v):
        c_core(v).wait_recv()
        put(v, o, precv[v])

    @pl.loop(0, nv)
    def _(v):
        c_x(v).wait_send()
        c_d2d(v).wait_send()
        c_fw(v).wait_send()

    @pl.loop(ne, nv)
    def _(v):
        c_core(v).wait_send()

    @pl.loop(0, ne)
    def _(v):
        c_e(v).wait_send()
        c_ef(v).wait_send()

    for k in range(np_):
        for f in (o_rs, o_ag, a_rs, a_ag):
            f(k).wait_send()
    for k in range(3):
        o_x(k).wait_send()
    for k in range(5):
        a_x(k).wait_send()
    g_own.wait_send()
    g_ab.wait_send()


def finish(f_ref, c_ref, fo_ref, co_ref, sems):
    copies = [pltpu.make_async_copy(c_ref, co_ref, sems.at[0]), pltpu.make_async_copy(f_ref, fo_ref, sems.at[1])]
    for copy in copies:
        copy.start()
    for copy in copies:
        copy.wait()


def per_device(nz, ny, fields, var_scale, start_basis):
    nv = fields.shape[0]
    x = fields.reshape(nv, 125, 2, 4, 128)
    ry = 128 // (nz * ny)
    np_ = nz * ny - 1
    block = (128, 4, 128)
    ne = min(4, nv - 1)
    dma = pltpu.SemaphoreType.DMA
    factor, core = pl.pallas_call(
        functools.partial(kernel, nv, ne, nz, ny),
        out_shape=(
            jax.ShapeDtypeStruct((64, 500), F32),
            jax.ShapeDtypeStruct((16 * nv * 8, 128), F32),
        ),
        in_specs=[
            pl.BlockSpec(memory_space=pltpu.SMEM),
            pl.BlockSpec(memory_space=pl.ANY),
            pl.BlockSpec(memory_space=pltpu.VMEM),
        ],
        out_specs=(pl.BlockSpec(memory_space=pltpu.VMEM), pl.BlockSpec(memory_space=pltpu.VMEM)),
        scratch_shapes=[
            pltpu.VMEM((nv, 2) + block, F32),
            pltpu.VMEM((nv, 2) + block, F32),
            pltpu.VMEM((nv,) + block, F32),
            pltpu.VMEM((nv,) + block, F32),
            pltpu.VMEM((ne,) + block, F32),
            pltpu.VMEM((ne,) + block, F32),
            pltpu.VMEM((nv, 512, 512), BF16),
            pltpu.VMEM((nv, 512, 512), BF16),
            pltpu.VMEM((ne + 1, 512, 512), BF16),
            pltpu.VMEM((ne + 1, 512, 512), BF16),
            pltpu.VMEM((128, 256), F32),
            pltpu.VMEM((2, 128, 128), F32),
            pltpu.VMEM((np_, ry, 256), F32),
            pltpu.VMEM((ry, 256), F32),
            pltpu.VMEM((2, 2, ry, 256), F32),
            pltpu.VMEM((np_, 2, ry, 128), F32),
            pltpu.VMEM((2, ry, 128), F32),
            pltpu.VMEM((2, 2, 2, ry, 128), F32),
            pltpu.VMEM((2, 256, 256), F32),
            pltpu.VMEM((2, 128, 128), F32),
            pltpu.VMEM((2, 128, 128), F32),
            pltpu.VMEM((768, 256), BF16),
            pltpu.VMEM((768, 256), BF16),
            pltpu.VMEM((64, 512), F32),
            pltpu.VMEM((64, 512), BF16),
            pltpu.VMEM((64, 512), BF16),
            pltpu.VMEM((nv, 16, 512), F32),
            pltpu.VMEM((nv, 16, 512), F32),
            dma((nv, 2)),
            dma((2, nv)),
            dma((2, nv)),
            dma((2, nv)),
            dma((2, ne)),
            dma((2, ne)),
            dma((2, 2 * np_ + 3)),
            dma((2, 2 * np_ + 5)),
            dma((2, 2)),
            dma((2, nv)),
        ],
        compiler_params=pltpu.CompilerParams(
            collective_id=0, has_side_effects=True, vmem_limit_bytes=60 * 1024 * 1024
        ),
        name="tucker",
    )(var_scale, x, start_basis.T)
    factor, core = pl.pallas_call(
        finish,
        out_shape=(jax.ShapeDtypeStruct((64, 500), F32), jax.ShapeDtypeStruct((16 * nv * 8, 128), F32)),
        in_specs=[pl.BlockSpec(memory_space=pltpu.VMEM)] * 2,
        out_specs=[pl.BlockSpec(memory_space=pl.ANY)] * 2,
        scratch_shapes=[dma((2,))],
        name="finish",
    )(factor, core)
    return factor.T, core.reshape(16, nv, 8, 128)


def solution(mesh):
    nz = mesh.shape["gy"]
    ny = mesh.shape["gz"] // 2
    in_specs = (P(None, "gx", "gy", "gz"), P(), P())
    out_specs = (P(), P("gx", None, "gy", "gz"))
    return jax.shard_map(
        functools.partial(per_device, nz, ny), mesh=mesh, in_specs=in_specs, out_specs=out_specs, check_vma=False
    )
```

time: 112 us -> 107 us (0.955)
  local copies, waits for them, and re-layouts: 3.58 us -> 0 us
  Pallas kernels: 108 us -> 106 us
    unnamed x2 -> x0, local copies, waits for them, and re-layouts: 3.58 us -> none
    pallas_call x1 -> x2, Pallas kernels: 108 us -> 106 us  [the longest x1 104 us: per_device(): pl.pallas_call(functools.partial(kernel, nv, ne, nz, ny), out_shape=(jax....]
where the time goes in v3:
time: 107 us
  Pallas kernels  106 us (99%)
    pallas_call x1, Pallas kernels, per_device(): pl.pallas_call(functools.partial(kernel, nv, ne, nz, ny), out_shape=(jax....  104 us

profile of v3, /device:TPU:1, one launch (start us, length us, event | category | flops | bytes accessed | tf_op | source)
XLA Modules:
  0.0 106.6 jit_solution(15423699485318385381)
XLA Ops:
  0.6 103.8 %tucker.1 = (f32[64,500]{1,0:T(8,128)}, f32[1408,128]{1,0:T(8,128)}) custom-call(f32[11]{0:T(128)} %scale_ref.1, f32[11,125,2,4,128]{4,3,2,1,0:T(4,128)} %bitcast.4, f32[64,500]{1,0:T(8,128)} %bitcast.5), custom_call_target="tpu_custom_call" | custom-call | tf_op jit(solution)/shard_map/tucker/pallas_call | solution.py:447
  104.5 2.1 %finish.1 = (f32[64,500]{1,0:T(8,128)}, f32[1408,128]{1,0:T(8,128)}) custom-call(f32[64,500]{1,0:T(8,128)} %get-tuple-element.6.f_ref, f32[1408,128]{1,0:T(8,128)} %get-tuple-element.7.c_ref), custom_call_target="tpu_custom_call" | custom-call | tf_op jit(solution)/shard_map/finish/pallas_call | solution.py:504

commit v4 on v3

--- a/solution.py
+++ b/solution.py
@@ -74,8 +74,8 @@
     xo, xd, xx, xf, xe, xg, Xh, Xl, Yh, Yl,
     acc_own, acc_ab,
     pb_o, b2_o, xb_o, pb_a, b2_a, xb_a,
-    gd, gk, gm, gh, gl, bt, fh, fl, psend, precv,
-    s_loc, s_d2d, s_x, s_fw, s_e, s_ef, s_ro, s_ra, s_g, s_c,
+    gd, gk, gm, gh, gl, first, bt, fh, fl, psend, precv,
+    s_loc, s_d2d, s_x, s_fw, s_e, s_ef, s_ro, s_ra, s_g, s_c, s_in,
 ):
     me = lax.axis_index("gx")
     z = lax.axis_index("gy")
@@ -92,6 +92,8 @@
 
     mate = dev(gx=2 * h + (1 - c))
     across = dev(gx=2 * o + c)
+    zline = [dev(gy=lax.rem(z + d, nz)) for d in range(1, nz)]
+    yline = [dev(yy=lax.rem(y + d, ny)) for d in range(1, ny)]
     np_ = nz * ny - 1
     spot = z * ny + y
     plane = []
@@ -133,7 +135,7 @@
         local(v, h).start()
 
     barrier = pltpu.get_barrier_semaphore()
-    greet = [mate] + [d for _, _, d in plane] + x_all + x_cross
+    greet = [mate, across, x_cross[0], x_hi] + zline + yline
     for d in greet:
         pl.semaphore_signal(barrier, inc=1, device_id=d, device_id_type=MESH)
     zero = jnp.zeros((3, 4, 128), F32)
@@ -147,6 +149,8 @@
         xe[v, 125:128] = zero
         xg[v, 125:128] = zero
     pl.semaphore_wait(barrier, len(greet))
+    for d in zline + [x_hi]:
+        pl.semaphore_signal(s_in, inc=1, device_id=d, device_id_type=MESH)
 
     ahead = min(4, nv)
 
@@ -251,6 +255,7 @@
 
     g_ab = rcopy(gk, gm, s_g, (1,), mate)
 
+    pl.semaphore_wait(s_in, len(zline) + 1)
     for k in range(np_):
         o_rs(k).start()
     steps = {1: own_1, 7: own_2, 9: own_3}
@@ -282,6 +287,21 @@
         def _():
             late(v - 1)
 
+    def halves(b):
+        bh, bl = split(b)
+        return (bh[:, 0:256], bl[:, 0:256]), (bh[:, 256:512], bl[:, 256:512])
+
+    def diagonal(b):
+        ba, bb = halves(b)
+        left = dot3(*ba, gh[0:256, :], gl[0:256, :], NN)
+        right = dot3(*bb, gh[256:512, :], gl[256:512, :], NN)
+        return jnp.concatenate([left, right], axis=1)
+
+    def crossing(b):
+        ba, bb = halves(b)
+        ax = gh[512:768, :], gl[512:768, :]
+        return jnp.concatenate([dot3(*bb, *ax, NT), dot3(*ba, *ax, NN)], axis=1)
+
     for k in range(np_):
         a_rs(k).start()
     c_e(0).start()
@@ -290,6 +310,7 @@
     g_own.wait_recv()
     gh[0:256], gl[0:256] = split(gd[0])
     gh[256:512], gl[256:512] = split(gd[1])
+    first[...] = diagonal(bt[...])
     for k in range(np_):
         a_rs(k).wait_recv()
     t = acc_ab[:, piece(0, spot), :]
@@ -331,23 +352,10 @@
     cc = lax.broadcasted_iota(jnp.int32, (64, 128), 1)
     eye = jnp.where(cc == rr + 64, 1.0, 0.0).astype(F32)
 
-    def times_gram(b):
-        bh, bl = split(b)
-        d0 = gh[0:256, :], gl[0:256, :]
-        d1 = gh[256:512, :], gl[256:512, :]
-        ax = gh[512:768, :], gl[512:768, :]
-        ba = bh[:, 0:256], bl[:, 0:256]
-        bb = bh[:, 256:512], bl[:, 256:512]
-        left = dot3(*ba, *d0, NN) + dot3(*bb, *ax, NT)
-        right = dot3(*ba, *ax, NN) + dot3(*bb, *d1, NN)
-        return jnp.concatenate([left, right], axis=1)
-
-    block = times_gram(bt[...])
+    block = first[...] + crossing(bt[...])
     for step in range(ITERS):
-        small = lax.dot_general(
-            block, jnp.concatenate([block, pad], axis=0), NT, precision=HI, preferred_element_type=F32
-        )
-        after = times_gram(block) if step < ITERS - 1 else block
+        small = dot3(*split(block), *split(jnp.concatenate([block, pad], axis=0)), NT)
+        after = diagonal(block) + crossing(block) if step < ITERS - 1 else block
         w = eliminate(small + eye)
         w = jnp.where(cc >= 64, w, 0.0)
         block = dot3(*split(w), *split(jnp.concatenate([pad, after], axis=0)), NN)
@@ -428,11 +436,19 @@
     g_ab.wait_send()
 
 
-def finish(f_ref, c_ref, fo_ref, co_ref, sems):
-    copies = [pltpu.make_async_copy(c_ref, co_ref, sems.at[0]), pltpu.make_async_copy(f_ref, fo_ref, sems.at[1])]
-    for copy in copies:
+def finish(f_ref, c_ref, fo_ref, co_ref, f_buf, c_buf, sems):
+    n = 4
+    size = c_ref.shape[0] // n
+    parts = [(c_ref.at[pl.ds(i * size, size)], c_buf.at[pl.ds(i * size, size)], co_ref.at[pl.ds(i * size, size)]) for i in range(n)]
+    parts.append((f_ref, f_buf, fo_ref))
+    reads = [pltpu.make_async_copy(a, b, sems.at[0, i]) for i, (a, b, _) in enumerate(parts)]
+    writes = [pltpu.make_async_copy(b, c, sems.at[1, i]) for i, (_, b, c) in enumerate(parts)]
+    for copy in reads:
         copy.start()
-    for copy in copies:
+    for read, write in zip(reads, writes):
+        read.wait()
+        write.start()
+    for copy in writes:
         copy.wait()
 
 
@@ -481,6 +497,7 @@
             pltpu.VMEM((768, 256), BF16),
             pltpu.VMEM((768, 256), BF16),
             pltpu.VMEM((64, 512), F32),
+            pltpu.VMEM((64, 512), F32),
             pltpu.VMEM((64, 512), BF16),
             pltpu.VMEM((64, 512), BF16),
             pltpu.VMEM((nv, 16, 512), F32),
@@ -495,6 +512,7 @@
             dma((2, 2 * np_ + 5)),
             dma((2, 2)),
             dma((2, nv)),
+            pltpu.SemaphoreType.REGULAR,
         ],
         compiler_params=pltpu.CompilerParams(
             collective_id=0, has_side_effects=True, vmem_limit_bytes=60 * 1024 * 1024
@@ -504,9 +522,9 @@
     factor, core = pl.pallas_call(
         finish,
         out_shape=(jax.ShapeDtypeStruct((64, 500), F32), jax.ShapeDtypeStruct((16 * nv * 8, 128), F32)),
-        in_specs=[pl.BlockSpec(memory_space=pltpu.VMEM)] * 2,
+        in_specs=[pl.BlockSpec(memory_space=pl.ANY)] * 2,
         out_specs=[pl.BlockSpec(memory_space=pl.ANY)] * 2,
-        scratch_shapes=[dma((2,))],
+        scratch_shapes=[pltpu.VMEM((64, 500), F32), pltpu.VMEM((16 * nv * 8, 128), F32), dma((2, 5))],
         name="finish",
     )(factor, core)
     return factor.T, core.reshape(16, nv, 8, 128)

time: 107 us -> 105 us (0.981)
  Pallas kernels: 106 us -> 104 us
    pallas_call x1, Pallas kernels: 104 us -> 102 us  [per_device(): pl.pallas_call(functools.partial(kernel, nv, ne, nz, ny), out_shape=(jax....]
where the time goes in v4:
time: 105 us
  Pallas kernels  104 us (99%)
    pallas_call x1, Pallas kernels, per_device(): pl.pallas_call(functools.partial(kernel, nv, ne, nz, ny), out_shape=(jax....  102 us

profile of v4, /device:TPU:1, one launch (start us, length us, event | category | flops | bytes accessed | tf_op | source)
XLA Modules:
  0.0 104.7 jit_solution(15058504351411943097)
XLA Ops:
  0.6 102.0 %tucker.1 = (f32[64,500]{1,0:T(8,128)}, f32[1408,128]{1,0:T(8,128)}) custom-call(f32[11]{0:T(128)} %scale_ref.1, f32[11,125,2,4,128]{4,3,2,1,0:T(4,128)} %bitcast.4, f32[64,500]{1,0:T(8,128)} %bitcast.5), custom_call_target="tpu_custom_call" | custom-call | tf_op jit(solution)/shard_map/tucker/pallas_call | solution.py:463
  102.7 2.0 %finish.1 = (f32[64,500]{1,0:T(8,128)}, f32[1408,128]{1,0:T(8,128)}) custom-call(f32[64,500]{1,0:T(8,128)} %get-tuple-element.6.f_ref, f32[1408,128]{1,0:T(8,128)} %get-tuple-element.7.c_ref), custom_call_target="tpu_custom_call" | custom-call | tf_op jit(solution)/shard_map/finish/pallas_call | solution.py:522
